TPU v7x, 16 devices: a 4x2x1 block of a 4x4x8 slice. The times are simulated.
16 devices in a mesh: rep: 4 (over y, z, core), pp: 4 (over x).
Axes of the slice: x: 4, y: 2, z: 1, core: 2. Of those that a mesh axis runs over, the one named last changes fastest.
The devices are a block of a 4x4x8 slice.
Arguments:
- x: bfloat16 [32, 512, 512], P('rep'), parts along dimension 0
- dy: bfloat16 [32, 512, 512], P('rep'), parts along dimension 0
- w_gate: bfloat16 [4, 512, 1408], P('pp')
- w_up: bfloat16 [4, 512, 1408], P('pp')
- w_down: bfloat16 [4, 1408, 512], P('pp')
Outputs:
- output 1: bfloat16 [16, 512, 1408], P(('rep', 'pp')), parts along dimension 0
- output 2: bfloat16 [16, 512, 1408], P(('rep', 'pp')), parts along dimension 0
- output 3: bfloat16 [16, 1408, 512], P(('rep', 'pp')), parts along dimension 0
There are 4 independent parts. A program takes and returns all parts, laid end to end along the dimension named above; an argument that names none is the same for every part.
All inputs are finite; a program needn't handle non-finite values.
Results may differ from a plain program's by a relative error of at most 0.018.
Values are sent between devices in bfloat16 or wider.
A program may use at most 768 MiB of HBM per device.

v0:
```python
import functools

import jax
import jax.numpy as jnp
from jax import lax
from jax.experimental import pallas as pl
from jax.experimental.pallas import tpu as pltpu
from jax.sharding import PartitionSpec as P

MESH = pl.DeviceIdType.MESH
F32, BF16 = jnp.float32, jnp.bfloat16
CHUNK = 128
LEAD = 4
OUT_SLOTS, BACK_SLOTS = 16, 8


def dot(a, b):
    return jnp.dot(a, b, preferred_element_type=F32)


def dot_tokens(a, b):
    return lax.dot_general(a, b, (((0,), (0,)), ((), ())), preferred_element_type=F32)


def rounded(v):
    return v.astype(BF16).astype(F32)


def kernel(
    n, x_ref, dy_ref, wg_ref, wu_ref, wd_ref, og_ref, ou_ref, od_ref,
    hbuf, dbuf, hout, dout, pbuf, qbuf, hid, dgu, abuf, wgu, wd, wgt, wut, wdt, accgu, accd,
    w_sem, hrecv, drecv, hsend, dsend, o_sem,
):
    micro, tokens, dim = x_ref.shape
    ff = wd_ref.shape[1]
    per = tokens // CHUNK
    chunks = micro * per
    slots, hid_micros = pbuf.shape[0], hid.shape[0]
    blocks = ff // 128
    me = lax.axis_index("pp")
    first, last = me == 0, me == n - 1
    lead = (n - 1 - me) * LEAD

    def rows_of(k):
        return k // per, pl.ds(pl.multiple_of((k % per) * CHUNK, CHUNK), CHUNK)

    def x_copy(k):
        m, rows = rows_of(k)
        return pltpu.make_async_copy(x_ref.at[m, rows], hbuf.at[m, rows], hrecv.at[k])

    def dy_copy(k):
        m, rows = rows_of(k)
        return pltpu.make_async_copy(dy_ref.at[m, rows], dbuf.at[m, rows], drecv.at[k])

    def h_copy(k):
        m, rows = rows_of(k)
        return pltpu.make_async_remote_copy(
            src_ref=hout.at[k % OUT_SLOTS], dst_ref=hbuf.at[m, rows], send_sem=hsend.at[k], recv_sem=hrecv.at[k],
            device_id={"pp": lax.rem(me + 1, n)}, device_id_type=MESH,
        )

    def d_copy(k):
        m, rows = rows_of(k)
        return pltpu.make_async_remote_copy(
            src_ref=dout.at[k % BACK_SLOTS], dst_ref=dbuf.at[m, rows], send_sem=dsend.at[k], recv_sem=drecv.at[k],
            device_id={"pp": lax.rem(me + n - 1, n)}, device_id_type=MESH,
        )

    loads = [pltpu.make_async_copy(wd_ref.at[0], wd, w_sem.at[2 * blocks])]
    for j in range(blocks):
        for i, ref in enumerate((wg_ref, wu_ref)):
            to = wgu.at[:, pl.ds(256 * j + 128 * i, 128)]
            loads.append(pltpu.make_async_copy(ref.at[0, :, pl.ds(128 * j, 128)], to, w_sem.at[2 * j + i]))

    @pl.when(first)
    def _():
        x_copy(0).start()

    for load in loads[1:] + loads[:1]:
        load.start()

    @pl.when(first)
    def _():
        @pl.loop(1, chunks)
        def _(k):
            x_copy(k).start()

    @pl.when(last)
    def _():
        @pl.loop(0, chunks)
        def _(k):
            dy_copy(k).start()

    barrier = pltpu.get_barrier_semaphore()

    @pl.when(me > 0)
    def _():
        pl.semaphore_signal(barrier, inc=1, device_id={"pp": lax.rem(me + n - 1, n)}, device_id_type=MESH)

    @pl.when(me < n - 1)
    def _():
        pl.semaphore_signal(barrier, inc=1, device_id={"pp": lax.rem(me + 1, n)}, device_id_type=MESH)

    pl.semaphore_wait(barrier, jnp.where(first, 0, 1) + jnp.where(last, 0, 1))

    for load in loads:
        load.wait()

    def prepare():
        for j in range(blocks):
            at = pl.ds(128 * j, 128)
            wgt[at, :] = wgu[:, pl.ds(256 * j, 128)].T
            wut[at, :] = wgu[:, pl.ds(256 * j + 128, 128)].T
            wdt[:, at] = wd[at, :].T
        accgu[...] = jnp.zeros_like(accgu)
        accd[...] = jnp.zeros_like(accd)

    def scaled(h):
        wide = h.astype(F32)
        scale = lax.rsqrt(jnp.mean(wide * wide, -1, keepdims=True) + 1e-6)
        return wide, scale, (wide * scale).astype(BF16)

    def forward(k):
        m, rows = rows_of(k)
        slot, hm = k % slots, m % hid_micros

        @pl.when(first)
        def _():
            x_copy(k).wait()

        @pl.when(me > 0)
        def _():
            h_copy(k).wait_recv()

        _, _, a = scaled(hbuf[m, rows, :])
        for j in range(blocks):
            both = dot(a, wgu[:, pl.ds(256 * j, 256)])
            gate, up = both[:, :128], both[:, 128:]
            s = jax.nn.sigmoid(gate)
            silu = gate * s
            at = pl.ds(128 * j, 128)
            pbuf[slot, :, at] = silu
            qbuf[slot, :, at] = up * (s + silu * (1.0 - s))
            hid[hm, rows, at] = (silu * up).astype(BF16)

        @pl.when(me < n - 1)
        def _():
            @pl.when(k >= OUT_SLOTS)
            def _():
                h_copy(k - OUT_SLOTS).wait_send()

            down = rounded(dot(hid[hm, rows, :], wd[...]))
            hout[k % OUT_SLOTS] = (hbuf[m, rows, :].astype(F32) + down).astype(BF16)
            h_copy(k).start()

    def backward(k):
        m, rows = rows_of(k)
        slot, two = k % slots, m % 2

        @pl.when(last)
        def _():
            dy_copy(k).wait()

        @pl.when(me < n - 1)
        def _():
            d_copy(k).wait_recv()

        dy = dbuf[m, rows, :]
        _, _, a = scaled(hbuf[m, rows, :])
        abuf[two, rows, :] = a
        for start in range(0, ff, 256):
            at = pl.ds(start, min(256, ff - start))
            dhid = rounded(dot(dy, wdt[:, at]))
            dgu[two, rows, at] = (dhid * qbuf[slot, :, at]).astype(BF16)
            dgu[two, rows, pl.ds(ff + start, min(256, ff - start))] = (dhid * pbuf[slot, :, at]).astype(BF16)

        @pl.when(me > 0)
        def _():
            @pl.when(k >= BACK_SLOTS)
            def _():
                d_copy(k - BACK_SLOTS).wait_send()

            by_gate = rounded(dot(dgu[two, rows, pl.ds(0, ff)], wgt[...]))
            by_up = rounded(dot(dgu[two, rows, pl.ds(ff, ff)], wut[...]))
            da = rounded(by_gate + by_up)
            wide, scale, _ = scaled(hbuf[m, rows, :])
            along = jnp.mean(da * wide, -1, keepdims=True)
            dn = rounded(da * scale - wide * (scale * scale * scale * along))
            dout[k % BACK_SLOTS] = (dbuf[m, rows, :].astype(F32) + dn).astype(BF16)
            d_copy(k).start()

    wide_tiles = 2 * ff // 256
    near = ff - 1024
    work = [
        [("gu", 256 * j, 256) for j in range(0, 4)],
        [("gu", 256 * j, 256) for j in range(4, 8)],
        [("gu", 256 * j, 256) for j in range(8, wide_tiles)] + [("d", 0, near)],
        [("d", near + 256 * i, 256) for i in range(4)],
    ]

    def weights(v):
        m, part = v // per, v % per
        two, hm = m % 2, m % hid_micros
        for number, items in enumerate(work):

            @pl.when(part == number)
            def _(items=items):
                for kind, start, size in items:
                    at = pl.ds(start, size)
                    if kind == "gu":
                        accgu[:, at] += rounded(dot_tokens(abuf[two], dgu[two, :, at]))
                    else:
                        accd[at, :] += rounded(dot_tokens(hid[hm, :, at], dbuf[m]))

    @pl.loop(0, chunks + lead + per)
    def _(t):
        @pl.when(t == jnp.where(first, lead, 0))
        def _():
            prepare()

        @pl.when(t < chunks)
        def _():
            forward(t)

        b = t - lead

        @pl.when((b >= 0) & (b < chunks))
        def _():
            backward(b)

        @pl.when(b >= per)
        def _():
            weights(b - per)

    outs = []

    def send_out(buffer, total, to):
        buffer[...] = total.astype(BF16)
        outs.append(pltpu.make_async_copy(buffer, to, o_sem.at[len(outs)]))
        outs[-1].start()

    for number, start in enumerate(range(0, ff, tokens)):
        at = pl.ds(start, min(tokens, ff - start))
        send_out(hbuf.at[number, pl.ds(0, at.size)], accd[at, :], od_ref.at[0, at])
    send_out(hid.at[0], accgu[:, pl.ds(0, ff)], og_ref.at[0])
    send_out(hid.at[1], accgu[:, pl.ds(ff, ff)], ou_ref.at[0])
    for copy in outs:
        copy.wait()

    @pl.when(me < n - 1)
    def _():
        @pl.loop(chunks - OUT_SLOTS, chunks)
        def _(k):
            h_copy(k).wait_send()

    @pl.when(me > 0)
    def _():
        @pl.loop(chunks - BACK_SLOTS, chunks)
        def _(k):
            d_copy(k).wait_send()


def solution(mesh):
    n = mesh.shape["pp"]

    def step(x, dy, w_gate, w_up, w_down):
        micro, tokens, dim = x.shape
        ff = w_down.shape[1]
        chunks = micro * (tokens // CHUNK)
        slots = (n - 1) * LEAD + 1
        any_space = pl.BlockSpec(memory_space=pl.ANY)
        return pl.pallas_call(
            functools.partial(kernel, n),
            out_shape=[jax.ShapeDtypeStruct(w.shape, BF16) for w in (w_gate, w_up, w_down)],
            in_specs=[any_space] * 5,
            out_specs=[any_space] * 3,
            scratch_shapes=[
                pltpu.VMEM((micro, tokens, dim), BF16),
                pltpu.VMEM((micro, tokens, dim), BF16),
                pltpu.VMEM((OUT_SLOTS, CHUNK, dim), BF16),
                pltpu.VMEM((BACK_SLOTS, CHUNK, dim), BF16),
                pltpu.VMEM((slots, CHUNK, ff), F32),
                pltpu.VMEM((slots, CHUNK, ff), F32),
                pltpu.VMEM((5, tokens, ff), BF16),
                pltpu.VMEM((2, tokens, 2 * ff), BF16),
                pltpu.VMEM((2, tokens, dim), BF16),
                pltpu.VMEM((dim, 2 * ff), BF16),
                pltpu.VMEM((ff, dim), BF16),
                pltpu.VMEM((ff, dim), BF16),
                pltpu.VMEM((ff, dim), BF16),
                pltpu.VMEM((dim, ff), BF16),
                pltpu.VMEM((dim, 2 * ff), F32),
                pltpu.VMEM((ff, dim), F32),
                pltpu.SemaphoreType.DMA((2 * (ff // 128) + 1,)),
                pltpu.SemaphoreType.DMA((chunks,)),
                pltpu.SemaphoreType.DMA((chunks,)),
                pltpu.SemaphoreType.DMA((chunks,)),
                pltpu.SemaphoreType.DMA((chunks,)),
                pltpu.SemaphoreType.DMA((-(-ff // tokens) + 2,)),
            ],
            compiler_params=pltpu.CompilerParams(collective_id=0, has_side_effects=True, vmem_limit_bytes=67_043_328),
        )(x, dy, w_gate, w_up, w_down)

    return jax.shard_map(
        step,
        mesh=mesh,
        in_specs=(P("rep", None, None),) * 2 + (P("pp", None, None),) * 3,
        out_specs=(P(("rep", "pp"), None, None),) * 3,
        check_vma=False,
    )
```

profile of v0, /device:TPU:112, one launch (start us, length us, event | category | flops | bytes accessed | tf_op | source)
XLA Modules:
  0.0 143.7 jit_solution(11119964806213506345)
XLA Ops:
  0.6 137.4 %shard_map.76 = (bf16[1,512,1408]{2,1,0:T(8,128)(2,1)}, bf16[1,512,1408]{2,1,0:T(8,128)(2,1)}, bf16[1,1408,512]{2,1,0:T(8,128)(2,1)}) custom-call(bf16[8,512,512]{2,1,0:T(8,128)(2,1)} %x_ref.1, bf16[8,512,512]{2,1,0:T(8,128)(2,1)} %dy_ref.1, bf16[1,512,1408]{2,1,0:T(8,128)(2,1)} %wg_ref.1, bf16[1,512,1408]{2,1,0:T(8,128)(2,1)} %wu_ref.1, ...), custom_call_target="tpu_custom_call" | custom-call | tf_op jit(solution)/shard_map/pallas_call | solution.py:272
  138.0 0.0 copy-start.1
  138.0 2.7 %copy.11 = bf16[1,512,1408]{2,1,0:T(8,128)(2,1)} copy(bf16[1,512,1408]{2,1,0:T(8,128)(2,1)} %get-tuple-element.6) | data formatting | bytes 2883584
  140.7 0.0 copy-done.1
  140.7 0.0 copy-start
  140.7 1.1 copy.12
  141.8 0.8 copy-done
  142.6 1.1 copy.13
Async XLA Ops:
  138.0 2.7 %copy-start.1 = (bf16[1,512,1408]{2,1,0:T(8,128)(2,1)S(1)}, bf16[1,512,1408]{2,1,0:T(8,128)(2,1)}, u32[]{:S(2)}) copy-start(bf16[1,512,1408]{2,1,0:T(8,128)(2,1)} %get-tuple-element.7) | copy-start | bytes 4325380
  140.7 1.9 %copy-start = (bf16[1,1408,512]{2,1,0:T(8,128)(2,1)S(1)}, bf16[1,1408,512]{2,1,0:T(8,128)(2,1)}, u32[]{:S(2)}) copy-start(bf16[1,1408,512]{2,1,0:T(8,128)(2,1)} %get-tuple-element.8) | copy-start | bytes 4325380
where the time goes:
time: 144 us
  Pallas kernels  137 us (95%)
  local copies, waits for them, and re-layouts  5.66 us (4%)
    pallas_call x1, Pallas kernels, step(): pl.pallas_call(functools.partial(kernel, n), out_shape=[jax.ShapeDtypeStr...  137 us
    unnamed x7, local copies, waits for them, and re-layouts  5.66 us

commit v1 on v0

v1 whole, which is shorter than its diff:
```python
import functools

import jax
import jax.numpy as jnp
from jax import lax
from jax.experimental import pallas as pl
from jax.experimental.pallas import tpu as pltpu
from jax.sharding import PartitionSpec as P

MESH = pl.DeviceIdType.MESH
F32, BF16 = jnp.float32, jnp.bfloat16
CHUNK = 128
HEAD, TAIL = (32, 32, 64), (64, 32, 32)
LEAD = 8
OUT_SLOTS, BACK_SLOTS = 16, 8


def dot(a, b):
    return jnp.dot(a, b, preferred_element_type=F32)


def dot_tokens(a, b):
    return lax.dot_general(a, b, (((0,), (0,)), ((), ())), preferred_element_type=F32)


def rounded(v):
    return v.astype(BF16).astype(F32)


def kernel(
    n, tokens, x_ref, dy_ref, wg_ref, wu_ref, wd_ref, og_ref, ou_ref, od_ref,
    hbuf, dbuf, hout, dout, pbuf, qbuf, hid, dgu, abuf, abuf_t, wgu, wd, wgt, wut, wdt, accgu, accd,
    w_sem, hrecv, drecv, hsend, dsend, o_sem,
):
    total, dim = x_ref.shape
    ff = wd_ref.shape[1]
    per = tokens // CHUNK
    heads, tails = len(HEAD), len(TAIL)
    units = total // CHUNK - 2 + heads + tails
    slots, hid_rows = pbuf.shape[0], hid.shape[0]
    blocks = ff // 128
    me = lax.axis_index("pp")
    first, last = me == 0, me == n - 1
    lead = ((n - 1 - me) * LEAD) // 2

    ends = [(k, sum(HEAD[:k]), size) for k, size in enumerate(HEAD)]
    ends += [(units - tails + k, total - CHUNK + sum(TAIL[:k]), size) for k, size in enumerate(TAIL)]

    def offset(k, size):
        off = (k - heads + 1) * CHUNK if size == CHUNK else 0
        for at, start, its in ends:
            if its == size:
                off = jnp.where(k == at, start, off)
        return pl.multiple_of(off, size)

    def is_size(k, size):
        if size == CHUNK:
            return (k >= heads) & (k < units - tails)
        found = False
        for at, _, its in ends:
            if its == size:
                found = (k == at) | found
        return found

    def per_size(k, body):
        for size in sorted({CHUNK, *HEAD, *TAIL}):

            @pl.when(is_size(k, size))
            def _(size=size):
                body(k, size, offset(k, size))

    def part_of(ref, off, size):
        return ref.at[pl.ds(pl.multiple_of(lax.rem(off, ref.shape[0]), size), size)]

    def x_copy(k, size, off):
        rows = pl.ds(off, size)
        return pltpu.make_async_copy(x_ref.at[rows], hbuf.at[rows], hrecv.at[k])

    def dy_copy(k, size, off):
        rows = pl.ds(off, size)
        return pltpu.make_async_copy(dy_ref.at[rows], dbuf.at[rows], drecv.at[k])

    def h_copy(k, size, off):
        return pltpu.make_async_remote_copy(
            src_ref=hout.at[lax.rem(k, OUT_SLOTS), pl.ds(0, size)], dst_ref=hbuf.at[pl.ds(off, size)],
            send_sem=hsend.at[k], recv_sem=hrecv.at[k], device_id={"pp": lax.rem(me + 1, n)}, device_id_type=MESH,
        )

    def d_copy(k, size, off):
        return pltpu.make_async_remote_copy(
            src_ref=dout.at[lax.rem(k, BACK_SLOTS), pl.ds(0, size)], dst_ref=dbuf.at[pl.ds(off, size)],
            send_sem=dsend.at[k], recv_sem=drecv.at[k], device_id={"pp": lax.rem(me + n - 1, n)}, device_id_type=MESH,
        )

    loads = []
    for j in range(blocks):
        for i, ref in enumerate((wg_ref, wu_ref)):
            to = wgu.at[:, pl.ds(256 * j + 128 * i, 128)]
            loads.append(pltpu.make_async_copy(ref.at[0, :, pl.ds(128 * j, 128)], to, w_sem.at[2 * j + i]))
    loads.append(pltpu.make_async_copy(wd_ref.at[0], wd, w_sem.at[2 * blocks]))

    barrier = pltpu.get_barrier_semaphore()

    @pl.when(me > 0)
    def _():
        pl.semaphore_signal(barrier, inc=1, device_id={"pp": lax.rem(me + n - 1, n)}, device_id_type=MESH)

    @pl.when(me < n - 1)
    def _():
        pl.semaphore_signal(barrier, inc=1, device_id={"pp": lax.rem(me + 1, n)}, device_id_type=MESH)

    @pl.when(first)
    def _():
        for at, start, size in ends[:heads]:
            x_copy(at, size, start).start()

    for load in loads:
        load.start()

    @pl.when(first)
    def _():
        @pl.loop(heads, units)
        def _(k):
            per_size(k, lambda *piece: x_copy(*piece).start())

    @pl.when(last)
    def _():
        @pl.loop(0, units)
        def _(k):
            per_size(k, lambda *piece: dy_copy(*piece).start())

    for load in loads:
        load.wait()
    pl.semaphore_wait(barrier, jnp.where(first, 0, 1) + jnp.where(last, 0, 1))

    def prepare():
        for j in range(blocks):
            at = pl.ds(128 * j, 128)
            wgt[at, :] = wgu[:, pl.ds(256 * j, 128)].T
            wut[at, :] = wgu[:, pl.ds(256 * j + 128, 128)].T
            wdt[:, at] = wd[at, :].T
        accgu[...] = jnp.zeros_like(accgu)
        accd[...] = jnp.zeros_like(accd)

    def scaled(h):
        wide = h.astype(F32)
        scale = lax.rsqrt(jnp.mean(wide * wide, -1, keepdims=True) + 1e-6)
        return wide, scale, (wide * scale).astype(BF16)

    def hidden(k, size, off):
        slot, hid_part = lax.rem(k, slots), part_of(hid, off, size)
        _, _, a = scaled(hbuf[pl.ds(off, size), :])
        for j in range(blocks):
            both = dot(a, wgu[:, pl.ds(256 * j, 256)])
            gate, up = both[:, :128], both[:, 128:]
            s = jax.nn.sigmoid(gate)
            silu = gate * s
            at = pl.ds(128 * j, 128)
            pbuf[slot, pl.ds(0, size), at] = silu
            qbuf[slot, pl.ds(0, size), at] = up * (s + silu * (1.0 - s))
            hid_part[:, at] = (silu * up).astype(BF16)

    def forward(k, size, off):
        @pl.when(first)
        def _():
            x_copy(k, size, off).wait()

        @pl.when(me > 0)
        def _():
            h_copy(k, size, off).wait_recv()

        @pl.when(k >= OUT_SLOTS)
        def _():
            per_size(k - OUT_SLOTS, lambda *piece: h_copy(*piece).wait_send())

        hidden(k, size, off)
        down = rounded(dot(part_of(hid, off, size)[...], wd[...]))
        hout[lax.rem(k, OUT_SLOTS), pl.ds(0, size), :] = (hbuf[pl.ds(off, size), :].astype(F32) + down).astype(BF16)
        h_copy(k, size, off).start()

    def backward_hidden(k, size, off):
        slot, rows, dgu_part = lax.rem(k, slots), pl.ds(off, size), part_of(dgu, off, size)
        dy = dbuf[rows, :]
        wide, scale, a = scaled(hbuf[rows, :])
        part_of(abuf, off, size)[...] = a
        for start in range(0, ff, 256):
            wide_by = min(256, ff - start)
            at = pl.ds(start, wide_by)
            dhid = rounded(dot(dy, wdt[:, at]))
            dgu_part[:, at] = (dhid * qbuf[slot, pl.ds(0, size), at]).astype(BF16)
            dgu_part[:, pl.ds(ff + start, wide_by)] = (dhid * pbuf[slot, pl.ds(0, size), at]).astype(BF16)
        return wide, scale

    def backward_input(k, size, off, wide, scale):
        dgu_part = part_of(dgu, off, size)
        by_gate = rounded(dot(dgu_part[:, pl.ds(0, ff)], wgt[...]))
        by_up = rounded(dot(dgu_part[:, pl.ds(ff, ff)], wut[...]))
        da = rounded(by_gate + by_up)
        along = jnp.mean(da * wide, -1, keepdims=True)
        dn = rounded(da * scale - wide * (scale * scale * scale * along))
        dout[lax.rem(k, BACK_SLOTS), pl.ds(0, size), :] = (dbuf[pl.ds(off, size), :].astype(F32) + dn).astype(BF16)
        d_copy(k, size, off).start()

    def back_slot_free(k):
        @pl.when(k >= BACK_SLOTS)
        def _():
            per_size(k - BACK_SLOTS, lambda *piece: d_copy(*piece).wait_send())

    def backward_first(k, size, off):
        d_copy(k, size, off).wait_recv()
        backward_hidden(k, size, off)

    def backward(k, size, off):
        d_copy(k, size, off).wait_recv()
        back_slot_free(k)
        backward_input(k, size, off, *backward_hidden(k, size, off))

    def forward_backward(k, size, off):
        dy_copy(k, size, off).wait()
        h_copy(k, size, off).wait_recv()
        back_slot_free(k)
        hidden(k, size, off)
        backward_input(k, size, off, *backward_hidden(k, size, off))

    down_near = 1024
    work = [
        [("d", 256 * i, 256) for i in range(down_near // 256)],
        [("d", down_near, ff - down_near)] + [("gu", 256 * j, 256) for j in range(0, 3)],
        [("gu", 256 * j, 256) for j in range(3, 7)],
        [("gu", 256 * j, 256) for j in range(7, 2 * ff // 256)],
    ]

    def weights(m, number, finish):
        two = pl.ds(pl.multiple_of(lax.rem(m, 2) * tokens, tokens), tokens)
        hid_at = pl.ds(pl.multiple_of(lax.rem(m * tokens, hid_rows), tokens), tokens)
        if number == 0:
            abuf_t[...] = abuf[two, :].T
        for kind, start, size in work[number]:
            at = pl.ds(start, size)
            if kind == "gu":
                term = rounded(dot(abuf_t[...], dgu[two, at]))
                ref, where = accgu, (slice(None), at)
            else:
                term = rounded(dot_tokens(hid[hid_at, at], dbuf[pl.ds(pl.multiple_of(m * tokens, tokens), tokens), :]))
                ref, where = accd, (at, slice(None))
            if finish is None:
                ref[where] += term
            else:
                finish(kind, start, size, ref[where] + term)

    @pl.loop(0, units + lead)
    def _(t):
        @pl.when(t == jnp.where(first, lead, 0))
        def _():
            prepare()

        @pl.when((t < units) & (me < n - 1))
        def _():
            per_size(t, forward)

        b = t - lead

        @pl.when((b >= 0) & first)
        def _():
            per_size(b, backward_first)

        @pl.when((b >= 0) & (me > 0) & (me < n - 1))
        def _():
            per_size(b, backward)

        @pl.when(last)
        def _():
            per_size(b, forward_backward)

        v = b - heads + 1 - per

        @pl.when((v >= 0) & (b <= units - tails))
        def _():
            for number in range(per):

                @pl.when(lax.rem(v, per) == number)
                def _(number=number):
                    weights(v // per, number, None)

    gate_out, up_out, down_out = hid.at[pl.ds(0, dim)], hid.at[pl.ds(dim, dim)], hbuf.at[pl.ds(0, ff)]
    outs = []

    def out(source, to):
        outs.append(pltpu.make_async_copy(source, to, o_sem.at[len(outs)]))
        outs[-1].start()

    def finish(kind, start, size, value):
        value = value.astype(BF16)
        if kind == "d":
            down_out[pl.ds(start, size), :] = value
            return
        for buffer, begin in ((gate_out, 0), (up_out, ff)):
            lo, hi = max(start, begin), min(start + size, begin + ff)
            if lo < hi:
                buffer[:, pl.ds(lo - begin, hi - lo)] = value[:, lo - start : hi - start]

    done = {"d": 0, "gu": 0}
    for number in range(per):
        weights(total // tokens - 1, number, finish)
        begun = dict(done)
        for kind, start, size in work[number]:
            done[kind] = start + size
        if done["d"] > begun["d"]:
            rows = pl.ds(begun["d"], done["d"] - begun["d"])
            out(down_out.at[rows], od_ref.at[0, rows])
        for buffer, to, begin in ((gate_out, og_ref, 0), (up_out, ou_ref, ff)):
            lo, hi = max(begun["gu"], begin), min(done["gu"], begin + ff)
            if lo < hi:
                columns = pl.ds(lo - begin, hi - lo)
                out(buffer.at[:, columns], to.at[0, :, columns])
    for copy in outs:
        copy.wait()

    @pl.when(me < n - 1)
    def _():
        @pl.loop(units - OUT_SLOTS, units)
        def _(k):
            per_size(k, lambda *piece: h_copy(*piece).wait_send())

    @pl.when(me > 0)
    def _():
        @pl.loop(units - BACK_SLOTS, units)
        def _(k):
            per_size(k, lambda *piece: d_copy(*piece).wait_send())


def copy_kernel(*refs):
    ins, outs, buffers, (in_sem, out_sem) = refs[:3], refs[3:6], refs[6:9], refs[9:]
    pieces = []
    for i, (source, to, buffer) in enumerate(zip(ins, outs, buffers, strict=True)):
        rows = source.shape[1] // 4
        for j in range(4):
            at = pl.ds(rows * j, rows)
            pieces.append((
                pltpu.make_async_copy(source.at[:, at], buffer.at[:, at], in_sem.at[4 * i + j]),
                pltpu.make_async_copy(buffer.at[:, at], to.at[:, at], out_sem.at[4 * i + j]),
            ))
    for come, _ in pieces:
        come.start()
    for come, go in pieces:
        come.wait()
        go.start()
    for _, go in pieces:
        go.wait()


def solution(mesh):
    n = mesh.shape["pp"]

    def step(x, dy, w_gate, w_up, w_down):
        micro, tokens, dim = x.shape
        ff = w_down.shape[1]
        total = micro * tokens
        units = total // CHUNK - 2 + len(HEAD) + len(TAIL)
        slots = (n - 1) * LEAD // 2 + 1
        any_space = pl.BlockSpec(memory_space=pl.ANY)
        shapes = [jax.ShapeDtypeStruct(w.shape, BF16) for w in (w_gate, w_up, w_down)]
        grads = pl.pallas_call(
            functools.partial(kernel, n, tokens),
            out_shape=shapes,
            in_specs=[any_space] * 5,
            out_specs=[any_space] * 3,
            scratch_shapes=[
                pltpu.VMEM((total, dim), BF16),
                pltpu.VMEM((total, dim), BF16),
                pltpu.VMEM((OUT_SLOTS, CHUNK, dim), BF16),
                pltpu.VMEM((BACK_SLOTS, CHUNK, dim), BF16),
                pltpu.VMEM((slots, CHUNK, ff), F32),
                pltpu.VMEM((slots, CHUNK, ff), F32),
                pltpu.VMEM((5 * tokens, ff), BF16),
                pltpu.VMEM((2 * tokens, 2 * ff), BF16),
                pltpu.VMEM((2 * tokens, dim), BF16),
                pltpu.VMEM((dim, tokens), BF16),
                pltpu.VMEM((dim, 2 * ff), BF16),
                pltpu.VMEM((ff, dim), BF16),
                pltpu.VMEM((ff, dim), BF16),
                pltpu.VMEM((ff, dim), BF16),
                pltpu.VMEM((dim, ff), BF16),
                pltpu.VMEM((dim, 2 * ff), F32),
                pltpu.VMEM((ff, dim), F32),
                pltpu.SemaphoreType.DMA((2 * (ff // 128) + 1,)),
                pltpu.SemaphoreType.DMA((units,)),
                pltpu.SemaphoreType.DMA((units,)),
                pltpu.SemaphoreType.DMA((units,)),
                pltpu.SemaphoreType.DMA((units,)),
                pltpu.SemaphoreType.DMA((8,)),
            ],
            compiler_params=pltpu.CompilerParams(collective_id=0, has_side_effects=True, vmem_limit_bytes=67_043_328),
        )(x.reshape(total, dim), dy.reshape(total, dim), w_gate, w_up, w_down)
        return pl.pallas_call(
            copy_kernel,
            out_shape=shapes,
            in_specs=[any_space] * 3,
            out_specs=[any_space] * 3,
            scratch_shapes=[pltpu.VMEM(s.shape, BF16) for s in shapes] + [pltpu.SemaphoreType.DMA((12,))] * 2,
            compiler_params=pltpu.CompilerParams(vmem_limit_bytes=67_043_328),
        )(*grads)

    return jax.shard_map(
        step,
        mesh=mesh,
        in_specs=(P("rep", None, None),) * 2 + (P("pp", None, None),) * 3,
        out_specs=(P(("rep", "pp"), None, None),) * 3,
        check_vma=False,
    )
```

time: 144 us -> 138 us (0.958)
  local copies, waits for them, and re-layouts: 5.66 us -> 0 us
    unnamed x7 -> x0, local copies, waits for them, and re-layouts: 5.66 us -> none
    pallas_call x1 -> x2, Pallas kernels: 137 us -> 137 us  [the longest x1 133 us: step(): pl.pallas_call(functools.partial(kernel, n, tokens), out_shape=shapes, in...]
where the time goes in v1:
time: 138 us
  Pallas kernels  137 us (99%)
    pallas_call x1, Pallas kernels, step(): pl.pallas_call(functools.partial(kernel, n, tokens), out_shape=shapes, in...  133 us
    pallas_call x1, Pallas kernels, step(): pl.pallas_call(copy_kernel, out_shape=shapes, in_specs=[any_space] * 3, o...  3.86 us

profile of v1, /device:TPU:112, one launch (start us, length us, event | category | flops | bytes accessed | tf_op | source)
XLA Modules:
  0.0 137.7 jit_solution(933196127793140289)
XLA Ops:
  0.6 133.1 %shard_map.76 = (bf16[1,512,1408]{2,1,0:T(8,128)(2,1)}, bf16[1,512,1408]{2,1,0:T(8,128)(2,1)}, bf16[1,1408,512]{2,1,0:T(8,128)(2,1)}) custom-call(bf16[4096,512]{1,0:T(8,128)(2,1)} %bitcast.2, bf16[4096,512]{1,0:T(8,128)(2,1)} %bitcast.3, bf16[1,512,1408]{2,1,0:T(8,128)(2,1)} %wg_ref.1, bf16[1,512,1408]{2,1,0:T(8,128)(2,1)} %wu_ref.1, ...), custom_call_target="tpu_custom_call" | custom-call | tf_op jit(solution)/shard_map/pallas_call | solution.py:363
  133.7 3.9 %shard_map.77 = (bf16[1,512,1408]{2,1,0:T(8,128)(2,1)}, bf16[1,512,1408]{2,1,0:T(8,128)(2,1)}, bf16[1,1408,512]{2,1,0:T(8,128)(2,1)}) custom-call(bf16[1,512,1408]{2,1,0:T(8,128)(2,1)} %get-tuple-element.6.refs_0_, bf16[1,512,1408]{2,1,0:T(8,128)(2,1)} %get-tuple-element.7.refs_1_, bf16[1,1408,512]{2,1,0:T(8,128)(2,1)} %get-tuple-element.8.refs_2_), custom_call_target="tpu_custom_call" | custom-call | tf_op jit(solution)/shard_map/pallas_call | solution.py:395

commit v2 on v1

--- a/solution.py
+++ b/solution.py
@@ -10,9 +10,9 @@
 MESH = pl.DeviceIdType.MESH
 F32, BF16 = jnp.float32, jnp.bfloat16
 CHUNK = 128
-HEAD, TAIL = (32, 32, 64), (64, 32, 32)
+HALF = CHUNK // 2
 LEAD = 8
-OUT_SLOTS, BACK_SLOTS = 16, 8
+OUT_SLOTS, BACK_SLOTS = 8, 8
 
 
 def dot(a, b):
@@ -30,47 +30,46 @@
 def kernel(
     n, tokens, x_ref, dy_ref, wg_ref, wu_ref, wd_ref, og_ref, ou_ref, od_ref,
     hbuf, dbuf, hout, dout, pbuf, qbuf, hid, dgu, abuf, abuf_t, wgu, wd, wgt, wut, wdt, accgu, accd,
-    w_sem, hrecv, drecv, hsend, dsend, o_sem,
+    w_sem, hrecv, drecv, hsend, dsend,
 ):
     total, dim = x_ref.shape
     ff = wd_ref.shape[1]
     per = tokens // CHUNK
-    heads, tails = len(HEAD), len(TAIL)
-    units = total // CHUNK - 2 + heads + tails
+    units = total // CHUNK + 1
     slots, hid_rows = pbuf.shape[0], hid.shape[0]
     blocks = ff // 128
     me = lax.axis_index("pp")
     first, last = me == 0, me == n - 1
     lead = ((n - 1 - me) * LEAD) // 2
 
-    ends = [(k, sum(HEAD[:k]), size) for k, size in enumerate(HEAD)]
-    ends += [(units - tails + k, total - CHUNK + sum(TAIL[:k]), size) for k, size in enumerate(TAIL)]
+    early = lax.rem(lax.axis_index("rep"), 2) == 0
+    other_half = jnp.where(early, 0, units - 2)
 
     def offset(k, size):
-        off = (k - heads + 1) * CHUNK if size == CHUNK else 0
-        for at, start, its in ends:
-            if its == size:
-                off = jnp.where(k == at, start, off)
-        return pl.multiple_of(off, size)
-
-    def is_size(k, size):
         if size == CHUNK:
-            return (k >= heads) & (k < units - tails)
-        found = False
-        for at, _, its in ends:
-            if its == size:
-                found = (k == at) | found
-        return found
+            return pl.multiple_of(k * CHUNK - jnp.where(early, HALF, 0), HALF)
+        return pl.multiple_of(jnp.where(k == units - 1, total - HALF, other_half * CHUNK), HALF)
 
     def per_size(k, body):
-        for size in sorted({CHUNK, *HEAD, *TAIL}):
-
-            @pl.when(is_size(k, size))
-            def _(size=size):
-                body(k, size, offset(k, size))
-
-    def part_of(ref, off, size):
-        return ref.at[pl.ds(pl.multiple_of(lax.rem(off, ref.shape[0]), size), size)]
+        is_half = (k == other_half) | (k == units - 1)
+
+        @pl.when(is_half)
+        def _():
+            body(k, HALF, offset(k, HALF))
+
+        @pl.when(jnp.logical_not(is_half))
+        def _():
+            body(k, CHUNK, offset(k, CHUNK))
+
+    def ring(ref, off, size):
+        return [ref.at[pl.ds(pl.multiple_of(lax.rem(off + at, ref.shape[0]), HALF), HALF)] for at in range(0, size, HALF)]
+
+    def put(parts, columns, value):
+        for number, part in enumerate(parts):
+            part[:, columns] = value[HALF * number : HALF * (number + 1)]
+
+    def get(parts, columns):
+        return jnp.concatenate([part[:, columns] for part in parts], 0)
 
     def x_copy(k, size, off):
         rows = pl.ds(off, size)
@@ -111,15 +110,14 @@
 
     @pl.when(first)
     def _():
-        for at, start, size in ends[:heads]:
-            x_copy(at, size, start).start()
+        per_size(0, lambda *piece: x_copy(*piece).start())
 
     for load in loads:
         load.start()
 
     @pl.when(first)
     def _():
-        @pl.loop(heads, units)
+        @pl.loop(1, units)
         def _(k):
             per_size(k, lambda *piece: x_copy(*piece).start())
 
@@ -148,7 +146,7 @@
         return wide, scale, (wide * scale).astype(BF16)
 
     def hidden(k, size, off):
-        slot, hid_part = lax.rem(k, slots), part_of(hid, off, size)
+        slot, hid_parts = lax.rem(k, slots), ring(hid, off, size)
         _, _, a = scaled(hbuf[pl.ds(off, size), :])
         for j in range(blocks):
             both = dot(a, wgu[:, pl.ds(256 * j, 256)])
@@ -158,7 +156,7 @@
             at = pl.ds(128 * j, 128)
             pbuf[slot, pl.ds(0, size), at] = silu
             qbuf[slot, pl.ds(0, size), at] = up * (s + silu * (1.0 - s))
-            hid_part[:, at] = (silu * up).astype(BF16)
+            put(hid_parts, at, (silu * up).astype(BF16))
 
     def forward(k, size, off):
         @pl.when(first)
@@ -174,27 +172,27 @@
             per_size(k - OUT_SLOTS, lambda *piece: h_copy(*piece).wait_send())
 
         hidden(k, size, off)
-        down = rounded(dot(part_of(hid, off, size)[...], wd[...]))
+        down = rounded(dot(get(ring(hid, off, size), pl.ds(0, ff)), wd[...]))
         hout[lax.rem(k, OUT_SLOTS), pl.ds(0, size), :] = (hbuf[pl.ds(off, size), :].astype(F32) + down).astype(BF16)
         h_copy(k, size, off).start()
 
     def backward_hidden(k, size, off):
-        slot, rows, dgu_part = lax.rem(k, slots), pl.ds(off, size), part_of(dgu, off, size)
+        slot, rows, dgu_parts = lax.rem(k, slots), pl.ds(off, size), ring(dgu, off, size)
         dy = dbuf[rows, :]
         wide, scale, a = scaled(hbuf[rows, :])
-        part_of(abuf, off, size)[...] = a
+        put(ring(abuf, off, size), pl.ds(0, dim), a)
         for start in range(0, ff, 256):
             wide_by = min(256, ff - start)
             at = pl.ds(start, wide_by)
             dhid = rounded(dot(dy, wdt[:, at]))
-            dgu_part[:, at] = (dhid * qbuf[slot, pl.ds(0, size), at]).astype(BF16)
-            dgu_part[:, pl.ds(ff + start, wide_by)] = (dhid * pbuf[slot, pl.ds(0, size), at]).astype(BF16)
+            put(dgu_parts, at, (dhid * qbuf[slot, pl.ds(0, size), at]).astype(BF16))
+            put(dgu_parts, pl.ds(ff + start, wide_by), (dhid * pbuf[slot, pl.ds(0, size), at]).astype(BF16))
         return wide, scale
 
     def backward_input(k, size, off, wide, scale):
-        dgu_part = part_of(dgu, off, size)
-        by_gate = rounded(dot(dgu_part[:, pl.ds(0, ff)], wgt[...]))
-        by_up = rounded(dot(dgu_part[:, pl.ds(ff, ff)], wut[...]))
+        dgu_parts = ring(dgu, off, size)
+        by_gate = rounded(dot(get(dgu_parts, pl.ds(0, ff)), wgt[...]))
+        by_up = rounded(dot(get(dgu_parts, pl.ds(ff, ff)), wut[...]))
         da = rounded(by_gate + by_up)
         along = jnp.mean(da * wide, -1, keepdims=True)
         dn = rounded(da * scale - wide * (scale * scale * scale * along))
@@ -272,9 +270,9 @@
         def _():
             per_size(b, forward_backward)
 
-        v = b - heads + 1 - per
-
-        @pl.when((v >= 0) & (b <= units - tails))
+        v = b - per
+
+        @pl.when((v >= 0) & (b <= units - 2))
         def _():
             for number in range(per):
 
@@ -282,39 +280,18 @@
                 def _(number=number):
                     weights(v // per, number, None)
 
-    gate_out, up_out, down_out = hid.at[pl.ds(0, dim)], hid.at[pl.ds(dim, dim)], hbuf.at[pl.ds(0, ff)]
-    outs = []
-
-    def out(source, to):
-        outs.append(pltpu.make_async_copy(source, to, o_sem.at[len(outs)]))
-        outs[-1].start()
-
     def finish(kind, start, size, value):
         value = value.astype(BF16)
         if kind == "d":
-            down_out[pl.ds(start, size), :] = value
+            od_ref[0, pl.ds(start, size), :] = value
             return
-        for buffer, begin in ((gate_out, 0), (up_out, ff)):
+        for ref, begin in ((og_ref, 0), (ou_ref, ff)):
             lo, hi = max(start, begin), min(start + size, begin + ff)
             if lo < hi:
-                buffer[:, pl.ds(lo - begin, hi - lo)] = value[:, lo - start : hi - start]
-
-    done = {"d": 0, "gu": 0}
+                ref[0, :, pl.ds(lo - begin, hi - lo)] = value[:, lo - start : hi - start]
+
     for number in range(per):
         weights(total // tokens - 1, number, finish)
-        begun = dict(done)
-        for kind, start, size in work[number]:
-            done[kind] = start + size
-        if done["d"] > begun["d"]:
-            rows = pl.ds(begun["d"], done["d"] - begun["d"])
-            out(down_out.at[rows], od_ref.at[0, rows])
-        for buffer, to, begin in ((gate_out, og_ref, 0), (up_out, ou_ref, ff)):
-            lo, hi = max(begun["gu"], begin), min(done["gu"], begin + ff)
-            if lo < hi:
-                columns = pl.ds(lo - begin, hi - lo)
-                out(buffer.at[:, columns], to.at[0, :, columns])
-    for copy in outs:
-        copy.wait()
 
     @pl.when(me < n - 1)
     def _():
@@ -330,23 +307,12 @@
 
 
 def copy_kernel(*refs):
-    ins, outs, buffers, (in_sem, out_sem) = refs[:3], refs[3:6], refs[6:9], refs[9:]
-    pieces = []
-    for i, (source, to, buffer) in enumerate(zip(ins, outs, buffers, strict=True)):
-        rows = source.shape[1] // 4
-        for j in range(4):
-            at = pl.ds(rows * j, rows)
-            pieces.append((
-                pltpu.make_async_copy(source.at[:, at], buffer.at[:, at], in_sem.at[4 * i + j]),
-                pltpu.make_async_copy(buffer.at[:, at], to.at[:, at], out_sem.at[4 * i + j]),
-            ))
-    for come, _ in pieces:
-        come.start()
-    for come, go in pieces:
-        come.wait()
-        go.start()
-    for _, go in pieces:
-        go.wait()
+    ins, outs, sem = refs[:3], refs[3:6], refs[6]
+    copies = [pltpu.make_async_copy(source, to, sem.at[i]) for i, (source, to) in enumerate(zip(ins, outs, strict=True))]
+    for copy in copies:
+        copy.start()
+    for copy in copies:
+        copy.wait()
 
 
 def solution(mesh):
@@ -356,15 +322,15 @@
         micro, tokens, dim = x.shape
         ff = w_down.shape[1]
         total = micro * tokens
-        units = total // CHUNK - 2 + len(HEAD) + len(TAIL)
+        units = total // CHUNK + 1
         slots = (n - 1) * LEAD // 2 + 1
         any_space = pl.BlockSpec(memory_space=pl.ANY)
         shapes = [jax.ShapeDtypeStruct(w.shape, BF16) for w in (w_gate, w_up, w_down)]
         grads = pl.pallas_call(
             functools.partial(kernel, n, tokens),
-            out_shape=shapes,
+            out_shape=[pltpu.VMEM(s.shape, BF16) for s in shapes],
             in_specs=[any_space] * 5,
-            out_specs=[any_space] * 3,
+            out_specs=[pl.BlockSpec(memory_space=pltpu.VMEM)] * 3,
             scratch_shapes=[
                 pltpu.VMEM((total, dim), BF16),
                 pltpu.VMEM((total, dim), BF16),
@@ -388,17 +354,16 @@
                 pltpu.SemaphoreType.DMA((units,)),
                 pltpu.SemaphoreType.DMA((units,)),
                 pltpu.SemaphoreType.DMA((units,)),
-                pltpu.SemaphoreType.DMA((8,)),
             ],
-            compiler_params=pltpu.CompilerParams(collective_id=0, has_side_effects=True, vmem_limit_bytes=67_043_328),
+            compiler_params=pltpu.CompilerParams(collective_id=0, has_side_effects=True, vmem_limit_bytes=62_600_000),
         )(x.reshape(total, dim), dy.reshape(total, dim), w_gate, w_up, w_down)
         return pl.pallas_call(
             copy_kernel,
             out_shape=shapes,
-            in_specs=[any_space] * 3,
+            in_specs=[pl.BlockSpec(memory_space=pltpu.VMEM)] * 3,
             out_specs=[any_space] * 3,
-            scratch_shapes=[pltpu.VMEM(s.shape, BF16) for s in shapes] + [pltpu.SemaphoreType.DMA((12,))] * 2,
-            compiler_params=pltpu.CompilerParams(vmem_limit_bytes=67_043_328),
+            scratch_shapes=[pltpu.SemaphoreType.DMA((3,))],
+            compiler_params=pltpu.CompilerParams(vmem_limit_bytes=1 << 20),
         )(*grads)
 
     return jax.shard_map(

time: 138 us -> 135 us (0.978)
  Pallas kernels: 137 us -> 134 us
    pallas_call x2, Pallas kernels: 137 us -> 134 us  [the longest x1 132 us: step(): pl.pallas_call(functools.partial(kernel, n, tokens), out_shape=[pltpu.VME...]
where the time goes in v2:
time: 135 us; the launch traced here: 134 us
  Pallas kernels  134 us (99%)
    pallas_call x1, Pallas kernels, step(): pl.pallas_call(functools.partial(kernel, n, tokens), out_shape=[pltpu.VME...  132 us

profile of v2, /device:TPU:112, one launch (start us, length us, event | category | flops | bytes accessed | tf_op | source)
XLA Modules:
  0.0 134.4 jit_solution(6505458527858747017)
XLA Ops:
  0.6 131.7 %shard_map.76 = (bf16[1,512,1408]{2,1,0:T(8,128)(2,1)S(1)}, bf16[1,512,1408]{2,1,0:T(8,128)(2,1)S(1)}, bf16[1,1408,512]{2,1,0:T(8,128)(2,1)S(1)}) custom-call(bf16[4096,512]{1,0:T(8,128)(2,1)} %bitcast.2, bf16[4096,512]{1,0:T(8,128)(2,1)} %bitcast.3, bf16[1,512,1408]{2,1,0:T(8,128)(2,1)} %wg_ref.1, bf16[1,512,1408]{2,1,0:T(8,128)(2,1)} %wu_ref.1, ...), custom_call_target="tpu_custom_call" | custom-call | tf_op jit(solution)/shard_map/pallas_call | solution.py:329
  132.3 2.1 %shard_map.77 = (bf16[1,512,1408]{2,1,0:T(8,128)(2,1)}, bf16[1,512,1408]{2,1,0:T(8,128)(2,1)}, bf16[1,1408,512]{2,1,0:T(8,128)(2,1)}) custom-call(bf16[1,512,1408]{2,1,0:T(8,128)(2,1)S(1)} %get-tuple-element.6.refs_0_, bf16[1,512,1408]{2,1,0:T(8,128)(2,1)S(1)} %get-tuple-element.7.refs_1_, bf16[1,1408,512]{2,1,0:T(8,128)(2,1)S(1)} %get-tuple-element.8.refs_2_), custom_call_target="tpu_custom_call" | custom-call | tf_op jit(solution)/shard_map/pallas_call | solution.py:360
